TPU v7x, 128 devices: a whole 4x4x4 slice. The times are simulated.
128 devices in a mesh: replica: 8 (over z, core), tp: 16 (over y, x).
Axes of the slice: x: 4, y: 4, z: 4, core: 2. Of those that a mesh axis runs over, the one named last changes fastest.
Arguments:
- hidden: bfloat16 [1024, 8192], P(('replica', 'tp')), may hold values from -64 to 64
- head: bfloat16 [152064, 8192], P(('replica', 'tp'))
- token_ids: int32 [1024], replicated, may hold values from 0 to 152063
Outputs:
- logprob: float32 [1024], P(('replica', 'tp'))
All inputs are finite; a program needn't handle non-finite values.
Results may differ from a plain program's by a relative error of at most 0.0003.
Values may be sent and summed in bfloat16 or wider, within the bound.
A program may use at most 128 MiB of HBM per device.

v0:
```python
import jax
import jax.numpy as jnp
from jax import lax
from jax.sharding import PartitionSpec as P


def in_one_piece(arrays, axis, split_dim, concat_dim, along):
    widths = [a.shape[along] for a in arrays]
    both = jnp.concatenate(arrays, axis=along)
    out = lax.all_to_all(both, axis, split_axis=split_dim, concat_axis=concat_dim, tiled=True)
    return tuple(jnp.split(out, [sum(widths[:k]) for k in range(1, len(widths))], axis=along))


def shards(hidden, head, token_ids):
    device_count = lax.axis_size("replica") * lax.axis_size("tp")
    per_device = hidden.shape[0]
    local_vocab = head.shape[0]
    position = lax.axis_index(("replica", "tp"))
    columns = position * local_vocab + jnp.arange(local_vocab, dtype=jnp.int32)
    gathered = lax.all_gather(hidden, ("replica", "tp"), axis=0, tiled=True)
    logits = lax.dot_general(
        gathered, head, (((1,), (1,)), ((), ())), preferred_element_type=jnp.float32
    )
    row_top = jnp.max(logits, axis=1)
    row_total = jnp.sum(jnp.exp(logits - row_top[:, None]), axis=1)
    row_picked = jnp.sum(jnp.where(columns[None, :] == token_ids[:, None], logits, 0.0), axis=1)
    stats = (row_top, row_total, row_picked)
    row_top, row_total, row_picked = stats
    shaped = (
        row_top.reshape(device_count, per_device),
        row_total.reshape(device_count, per_device),
        row_picked.reshape(device_count, per_device),
    )
    arrived = in_one_piece((shaped[0], shaped[1], shaped[2]), ("replica", "tp"), 0, 0, 1)
    final_top = jnp.max(arrived[0], axis=0)
    final_total = jnp.sum(arrived[1] * jnp.exp(arrived[0] - final_top[None, :]), axis=0)
    final_picked = jnp.sum(arrived[2], axis=0)
    return final_picked - final_top - jnp.log(final_total)


def solution(mesh):
    in_specs = (P(("replica", "tp"), None), P(("replica", "tp"), None), P())
    out_specs = P(("replica", "tp"))
    return jax.shard_map(shards, mesh=mesh, in_specs=in_specs, out_specs=out_specs, check_vma=False)
```

profile of v0, /device:TPU:1, one launch (start us, length us, event | category | flops | bytes accessed | tf_op | source)
XLA Modules:
  0.0 149.2 jit_solution(16097349257414862518)
XLA Ops:
  6.5 0.0 all-gather.2.cloned.1.call-start
  6.5 0.7 all-gather.2.cloned.1.call-update
  7.3 0.0 copy-start
  7.3 86.8 %all-gather.2.cloned.1.call-done = bf16[1024,8192]{1,0:T(8,128)(2,1)} async-done(((bf16[8,8192]{1,0:T(8,128)(2,1)}), bf16[1024,8192]{1,0:T(8,128)(2,1)}) %all-gather.2.cloned.1.call-update) | async-done | bytes 16777232 | tf_op jit(solution)/shard_map/all_gather | solution.py:20
  94.1 27.3 %fusion.1 = (f32[1024]{0:T(1024)S(1)}, f32[1024,1188]{0,1:T(8,128)}) fusion(bf16[1024,8192]{1,0:T(8,128)(2,1)} %all-gather.2.cloned.1.call-done, bf16[1188,8192]{1,0:T(8,128)(2,1)} %param.4), kind=kOutput, calls=%fused_computation.9 | convolution fusion | flops 19932549120 | bytes 41111552 | tf_op jit(solution)/shard_map/dot_general | solution.py:21
  121.4 0.1 reshape.18
  121.5 0.0 copy-done
  121.5 3.1 %exponential_reduce_fusion = (f32[1024]{0:T(1024)S(1)}, f32[1024]{0:T(1024)S(1)}) fusion(f32[1024,1188]{0,1:T(8,128)} %get-tuple-element.10, f32[1024]{0:T(1024)S(1)} %get-tuple-element.9, s32[1024]{0:T(1024)S(1)} %copy-done, s32[1188]{0:T(1024)S(1)} %iota_add_fusion), kind=kLoop, calls=%fused_computation.1 | loop fusion | flops 6080512 | bytes 4887184 | tf_op jit(solution)/shard_map/reduce_sum | solution.py:25
  124.6 0.1 reshape.19
  124.7 0.1 reshape.20
  124.8 0.1 pad_maximum_fusion
  124.9 16.8 %all_to_all.12 = f32[128,1,24]{2,1,0:T(1,128)S(1)} all-to-all(f32[128,1,24]{2,1,0:T(1,128)S(1)} %bitcast.8), channel_id=1, replica_groups=mesh['replica'=8,'tp'=16] {'replica','tp'}, dimensions={0} | all-to-all | bytes 24576 | tf_op jit(solution)/shard_map/all_to_all | solution.py:10
  141.8 0.1 slice_reduce_fusion
  141.9 0.5 log_subtract_fusion
  (2 shorter events, 0.0 us)
Async XLA Ops:
  6.5 87.6 %all-gather.2.cloned.1.call-start = ((), (), s32[]{:S(2)}) async-start(), calls=%async_computation.1 | async-start | bytes 16908288 | tf_op jit(solution)/shard_map/all_gather | solution.py:20
  7.3 114.2 %copy-start = (s32[1024]{0:T(1024)S(1)}, s32[1024]{0:T(1024)}, u32[]{:S(2)}) copy-start(s32[1024]{0:T(1024)} %param.5) | copy-start | bytes 12292
Sparse Core Ops, SparseCore 0:
  10.5 83.5 all-gather.1
where the time goes:
time: 149 us
  waiting for transfers between devices  87.5 us (59%)
  matrix products  27.3 us (18%)
  blocking collectives  16.8 us (11%)
  between operations  13.5 us (9%)
  other arithmetic  3.93 us (3%)
    all_gather x1, waiting for transfers between devices, shards(): gathered = lax.all_gather(hidden, ('replica', 'tp'), axis=0, tiled=True)  86.8 us
    dot_general x1, matrix products, shards(): lax.dot_general(gathered, head, (((1,), (1,)), ((), ())), preferred_eleme...  27.3 us
    all_to_all x1, blocking collectives, in_one_piece(): lax.all_to_all(both, axis, split_axis=split_dim, concat_axis=concat_dim,...  16.8 us
    reduce_sum x1, other arithmetic, shards(): row_total = jnp.sum(jnp.exp(logits - row_top[:, None]), axis=1)  3.15 us
  transfers between devices with their start and end apart: 1, of which 1 were waited for; matrix products, arithmetic and copies ran while one was open for 0% of the time, Pallas kernels for 0%

commit v1 on v0

--- a/solution.py
+++ b/solution.py
@@ -17,7 +17,9 @@
     local_vocab = head.shape[0]
     position = lax.axis_index(("replica", "tp"))
     columns = position * local_vocab + jnp.arange(local_vocab, dtype=jnp.int32)
-    gathered = lax.all_gather(hidden, ("replica", "tp"), axis=0, tiled=True)
+    local_now = jnp.stack([hidden] * jax.lax.psum(1, ("replica", "tp")))
+    reached = jax.lax.all_to_all(local_now, ("replica", "tp"), 0, 0)
+    gathered = jnp.concatenate(reached, axis=0)
     logits = lax.dot_general(
         gathered, head, (((1,), (1,)), ((), ())), preferred_element_type=jnp.float32
     )

time: 149 us -> 319 us (2.14)
  waiting for transfers between devices: 87.5 us -> 227 us
  blocking collectives: 16.8 us -> 42.1 us
  between operations: 13.5 us -> 0.08 us
  starting transfers between devices: 0.01 us -> 11.9 us
  local copies, waits for them, and re-layouts: 0.25 us -> 6.95 us
    all_to_all x0 -> x1, waiting for transfers between devices: none -> 227 us  [shards(): reached = jax.lax.all_to_all(local_now, ('replica', 'tp'), 0, 0)]
    all_gather x1 -> x0, waiting for transfers between devices: 86.8 us -> none  [shards(): gathered = lax.all_gather(hidden, ('replica', 'tp'), axis=0, tiled=True)]
    all_to_all x1, blocking collectives: 16.8 us -> 42.1 us  [in_one_piece(): lax.all_to_all(both, axis, split_axis=split_dim, concat_axis=concat_dim,...]
    all_to_all x0 -> x1, starting transfers between devices: none -> 11.9 us  [shards(): reached = jax.lax.all_to_all(local_now, ('replica', 'tp'), 0, 0)]
    another operation x0 -> x1, local copies, waits for them, and re-layouts: none -> 6.71 us  [shards(): local_now = jnp.stack([hidden] * jax.lax.psum(1, ('replica', 'tp')))]
where the time goes in v1:
time: 319 us
  waiting for transfers between devices  227 us (71%)
  blocking collectives  42.1 us (13%)
  matrix products  27.3 us (9%)
  starting transfers between devices  11.9 us (4%)
  local copies, waits for them, and re-layouts  6.95 us (2%)
  other arithmetic  3.93 us (1%)
    all_to_all x1, waiting for transfers between devices, shards(): reached = jax.lax.all_to_all(local_now, ('replica', 'tp'), 0, 0)  227 us
    all_to_all x1, blocking collectives, in_one_piece(): lax.all_to_all(both, axis, split_axis=split_dim, concat_axis=concat_dim,...  42.1 us
    dot_general x1, matrix products, shards(): lax.dot_general(gathered, head, (((1,), (1,)), ((), ())), preferred_eleme...  27.3 us
    all_to_all x1, starting transfers between devices, shards(): reached = jax.lax.all_to_all(local_now, ('replica', 'tp'), 0, 0)  11.9 us
    another operation x1, local copies, waits for them, and re-layouts, shards(): local_now = jnp.stack([hidden] * jax.lax.psum(1, ('replica', 'tp')))  6.71 us
  transfers between devices with their start and end apart: 1, of which 1 were waited for; matrix products, arithmetic and copies ran while one was open for 0% of the time, Pallas kernels for 0%

profile of v1, /device:TPU:1, one launch (start us, length us, event | category | flops | bytes accessed | tf_op | source)
XLA Modules:
  0.0 319.1 jit_solution(5169966854912995596)
XLA Ops:
  0.0 6.7 %stack.2 = bf16[128,8,8192]{2,1,0:T(8,128)(2,1)} broadcast(bf16[8,8192]{1,0:T(8,128)(2,1)} %param.3), dimensions={1,2} | broadcast | bytes 16908288 | tf_op jit(solution)/shard_map/stack | solution.py:20
  6.7 11.9 %all-to-all-start = ((bf16[128,8,8192]{2,1,0:T(8,128)(2,1)}), bf16[128,8,8192]{2,1,0:T(8,128)(2,1)}, u32[]{:S(2)}, u32[]{:S(2)}) async-start(bf16[128,8,8192]{2,1,0:T(8,128)(2,1)} %stack.2), calls=%async_computation | async-start | bytes 33554432 | tf_op jit(solution)/shard_map/all_to_all | solution.py:21
  18.7 0.0 copy-start
  18.7 226.8 %all-to-all-done = bf16[128,8,8192]{2,1,0:T(8,128)(2,1)} async-done(((bf16[128,8,8192]{2,1,0:T(8,128)(2,1)}), bf16[128,8,8192]{2,1,0:T(8,128)(2,1)}, u32[]{:S(2)}, u32[]{:S(2)}) %all-to-all-start) | async-done | bytes 16777248 | tf_op jit(solution)/shard_map/all_to_all | solution.py:21
  245.5 27.3 %fusion.3 = (f32[1024]{0:T(1024)S(1)}, f32[1024,1188]{0,1:T(8,128)}) fusion(bf16[1188,8192]{1,0:T(8,128)(2,1)} %param.4, bf16[128,8,8192]{2,1,0:T(8,128)(2,1)} %all-to-all-done), kind=kOutput, calls=%fused_computation.11 | convolution fusion | flops 19932549120 | bytes 41111552 | tf_op jit(solution)/shard_map/dot_general | solution.py:23
  272.8 0.1 reshape.24
  272.8 0.0 copy-done
  272.9 3.1 exponential_reduce_fusion
  276.0 0.1 reshape.25
  276.1 0.1 reshape.26
  276.2 0.1 pad_maximum_fusion
  276.3 42.1 %all_to_all.17 = f32[128,1,24]{2,1,0:T(1,128)S(1)} all-to-all(f32[128,1,24]{2,1,0:T(1,128)S(1)} %bitcast.12), channel_id=1, replica_groups=mesh['replica'=8,'tp'=16] {'replica','tp'}, dimensions={0} | all-to-all | bytes 24576 | tf_op jit(solution)/shard_map/all_to_all | solution.py:10
  318.4 0.1 slice_reduce_fusion
  318.5 0.5 log_subtract_fusion
  (2 shorter events, 0.0 us)
Async XLA Ops:
  6.7 238.8 %all-to-all-start = ((bf16[128,8,8192]{2,1,0:T(8,128)(2,1)}), bf16[128,8,8192]{2,1,0:T(8,128)(2,1)}, u32[]{:S(2)}, u32[]{:S(2)}) async-start(bf16[128,8,8192]{2,1,0:T(8,128)(2,1)} %stack.2), calls=%async_computation | async-start | bytes 33554432 | tf_op jit(solution)/shard_map/all_to_all | solution.py:21
  18.7 254.2 %copy-start = (s32[1024]{0:T(1024)S(1)}, s32[1024]{0:T(1024)}, u32[]{:S(2)}) copy-start(s32[1024]{0:T(1024)} %param.5) | copy-start | bytes 12292
